TPU v7x, 32 devices: a whole 2x2x4 slice. The times are simulated.
32 devices in a mesh: img: 8 (over y, x, core), atom: 4 (over z).
Axes of the slice: x: 2, y: 2, z: 4, core: 2. Of those that a mesh axis runs over, the one named last changes fastest.
Arguments:
- positions: float32 [3, 256, 4096], P(None, 'img', 'atom'), may hold values from -6 to 6
- strength: float32 [4096], replicated, may hold values from 0.5 to 2
- tile_pairs: int32 [32, 8], replicated, may hold values from 0 to 31
- source_segment: int32 [256], P('img'), may hold values from 1 to 255, as said below
Outputs:
- string: float32 [3, 256, 4096], P(None, 'img', 'atom')
Inputs may be any that keep to these rules, and one draw needn't show every extreme that they name: source_segment[j] is j or j + 1, never 0 and never above 255.
All inputs are finite; a program needn't handle non-finite values.
Results may differ from a plain program's by a relative error of at most 0.0003.
Values sent between devices are 32-bit elements; how exact they have to be, the bound alone decides.
No kernel may reach another device: no remote copies, remote signals or barrier semaphores. Data moves between devices by JAX's collectives and lax.ppermute only.
A program may use at most 64 MiB of HBM per device.

v0:
```python
import jax
import jax.numpy as jnp
from jax import lax
from jax.sharding import PartitionSpec as P

TB = 128
STEP_SIZE = 0.02


def padded(cells, sides, width):
    for axis, dim in sides:
        count = lax.axis_size(axis)
        ends = count - 1
        head = lax.slice_in_dim(cells, 0, width, axis=dim)
        tail = lax.slice_in_dim(cells, cells.shape[dim] - width, cells.shape[dim], axis=dim)
        cells = jnp.concatenate(
            [
                lax.ppermute(tail, axis, [(i, (i + 1) % count) for i in range(ends)]),
                cells,
                lax.ppermute(head, axis, [((i + 1) % count, i) for i in range(ends)]),
            ],
            axis=dim,
        )
    return cells


def pair_force(block_pos, block_strength, whole_pos, strength, partners):
    force_sum = jnp.zeros(block_pos.shape, jnp.float32)
    for neighbor_slot in range(partners.shape[0]):
        first_atom = partners[neighbor_slot] * TB
        partner_pos = lax.dynamic_slice_in_dim(whole_pos, first_atom, TB, 2)
        partner_strength = lax.dynamic_slice_in_dim(strength, first_atom, TB, 0)
        differ = block_pos[:, :, :, None] - partner_pos[:, :, None, :]
        radius = jnp.sum(differ * differ, axis=0)
        coupling = (
            block_strength[None, :, None] * partner_strength[None, None, :] * jnp.exp(-0.5 * radius)
        )
        force_sum = force_sum + jnp.sum(differ * coupling[None], axis=3)
    return force_sum


def block_forces(blocks, indices, strength, tile_pairs, whole_pos):

    def one_block(inputs):
        block_pos, index = inputs
        partners = tile_pairs[index]
        block_strength = lax.dynamic_slice_in_dim(strength, index * TB, TB, 0)
        return pair_force(block_pos, block_strength, whole_pos, strength, partners)

    result = lax.map(one_block, (blocks, indices))
    block_count, _, image_count, _ = result.shape
    return result.transpose(1, 2, 0, 3).reshape(3, image_count, block_count * TB)


def shards(positions, strength, tile_pairs, source_segment):
    count = positions.shape[1]
    local_atoms = positions.shape[2]
    whole_pos = lax.all_gather(positions, "atom", axis=2, tiled=True)
    per_device = local_atoms // TB
    blocks = positions.reshape(3, count, per_device, TB).transpose(2, 0, 1, 3)
    indices = lax.axis_index("atom") * per_device + jnp.arange(per_device, dtype=jnp.int32)
    forces = block_forces(blocks, indices, strength, tile_pairs, whole_pos)
    moved = positions + STEP_SIZE * forces
    first_image = lax.axis_index("img") * count
    images_total = count * lax.axis_size("img")
    extended = padded(moved, (("img", 1),), 1)
    segments = extended[:, 1:] - extended[:, :-1]
    partial_value = jnp.sum(segments * segments, axis=(0, 2))
    squares = lax.psum(partial_value, "atom")
    global_ids = first_image + jnp.arange(count + 1, dtype=jnp.int32)
    valid = (global_ids >= 1) & (global_ids <= images_total - 1)
    lengths = jnp.where(valid, jnp.sqrt(1.0 + squares), jnp.zeros_like(squares))
    running = jnp.cumsum(lengths[:count])
    device_total = running[-1]
    totals = lax.all_gather(device_total[None], "img", axis=0, tiled=True)
    ranks = jnp.arange(totals.shape[0], dtype=jnp.int32)
    offset = jnp.sum(jnp.where(ranks < lax.axis_index("img"), totals, jnp.zeros_like(totals)))
    total_arc = jnp.sum(totals)
    arc_ext = jnp.concatenate(
        [offset[None], offset + running, (offset + device_total + lengths[count])[None]]
    )
    length_ext = jnp.concatenate([jnp.zeros((1,), jnp.float32), lengths])
    upper = source_segment - first_image + 1
    lower = upper - 1
    columns = jnp.arange(count + 2, dtype=jnp.int32)
    hit_low = (columns[None, :] == lower[:, None]).astype(jnp.float32)
    hit_high = (columns[None, :] == upper[:, None]).astype(jnp.float32)
    arc_low = jnp.sum(hit_low * arc_ext[None, :], axis=1)
    seg_length = jnp.sum(hit_high * length_ext[None, :], axis=1)
    target = (first_image + jnp.arange(count, dtype=jnp.int32)).astype(jnp.float32) * (
        total_arc / (images_total - 1)
    )
    weight = (target - arc_low) / seg_length
    mixing = (1.0 - weight)[:, None] * hit_low + weight[:, None] * hit_high
    string = jnp.einsum("je,cea->cja", mixing, extended, precision=lax.Precision.HIGHEST)
    return string


def solution(mesh):
    placed = (P(None, "img", "atom"), P(), P(), P("img"))
    return jax.shard_map(
        shards, mesh=mesh, in_specs=placed, out_specs=P(None, "img", "atom"), check_vma=False
    )
```

profile of v0, /device:TPU:4, one launch (start us, length us, event | category | flops | bytes accessed | tf_op | source)
XLA Modules:
  0.0 445.7 jit_solution(13500189040580754193)
XLA Ops:
  7.3 1.1 copy.15
  8.4 38.8 %all-gather.3.cloned.1.call-done = f32[3,32,4096]{2,1,0:T(8,128)} async-done(((f32[3,32,1024]{2,1,0:T(8,128)}), f32[3,32,4096]{2,1,0:T(8,128)}) %all-gather.3.cloned.1.call-update) | async-done | bytes 1572880 | tf_op jit(solution)/shard_map/all_gather | solution.py:58
  47.2 351.6 %while.10 = (s32[]{:T(128)}, f32[8,3,32,128]{3,2,1,0:T(8,128)}, f32[8,3,32,128]{3,0,2,1:T(8,128)S(1)}, s32[8]{0:T(128)S(1)}, s32[32,8]{0,1:T(8,128)}, /*index=5*...) while((s32[]{:T(128)}, f32[8,3,32,128]{3,2,1,0:T(8,128)}, ...), condition=%wide.region_17.18_spmd, body=%wide.region_0.17_spmd.sunk | while | flops 79810600 | bytes 70826768 | solution.py:50
  55.8 1.0 constant_dynamic-slice_fusion.14
  56.9 3.7 fusion.45
  62.3 2.1 exponential_multiply_fusion.15
  64.4 10.2 %fusion.47 = (f32[3,32,128]{2,1,0:T(8,128)S(1)}, f32[32,128,128]{2,1,0:T(8,128)S(1)}, f32[32,128,128]{2,1,0:T(8,128)S(1)}, f32[32,128,128]{2,1,0:T(8,128)S(1)}, ...) fusion(f32[32,128,128]{2,1,0:T(8,128)S(1)} %get-tuple-element.2, ...), kind=kLoop, calls=%fused_computation.19.clone.1 | loop fusion | flops 34578432 | bytes 17317888 | tf_op jit(solution)/shard_map/while/body/eval_jaxpr/reduce_sum | solution.py:38
  76.3 14.1 %fusion.48 = (f32[3,32,128]{2,1,0:T(8,128)S(1)}, f32[3,32,128]{2,1,0:T(8,128)S(1)}, f32[3,32,128]{2,1,0:T(8,128)S(1)}, f32[3,32,128]{2,1,0:T(8,128)S(1)}, f32[3,...) fusion(f32[32,128,128]{2,1,0:T(8,128)S(1)} %exponential_multiply_fusion.16, ...), kind=kLoop, calls=%fused_computation.21.clone.1 | loop fusion | flops 28237824 | bytes 13221888 | tf_op jit(solution)/shard_map/while/body/eval_jaxpr/reduce_sum | solution.py:38
  100.9 3.7 fusion.45
  106.2 2.1 exponential_multiply_fusion.15
  108.4 10.2 %fusion.47 = (f32[3,32,128]{2,1,0:T(8,128)S(1)}, f32[32,128,128]{2,1,0:T(8,128)S(1)}, f32[32,128,128]{2,1,0:T(8,128)S(1)}, f32[32,128,128]{2,1,0:T(8,128)S(1)}, ...) fusion(f32[32,128,128]{2,1,0:T(8,128)S(1)} %get-tuple-element.2, ...), kind=kLoop, calls=%fused_computation.19.clone.1 | loop fusion | flops 34578432 | bytes 17317888 | tf_op jit(solution)/shard_map/while/body/eval_jaxpr/reduce_sum | solution.py:38
  120.3 14.1 %fusion.48 = (f32[3,32,128]{2,1,0:T(8,128)S(1)}, f32[3,32,128]{2,1,0:T(8,128)S(1)}, f32[3,32,128]{2,1,0:T(8,128)S(1)}, f32[3,32,128]{2,1,0:T(8,128)S(1)}, f32[3,...) fusion(f32[32,128,128]{2,1,0:T(8,128)S(1)} %exponential_multiply_fusion.16, ...), kind=kLoop, calls=%fused_computation.21.clone.1 | loop fusion | flops 28237824 | bytes 13221888 | tf_op jit(solution)/shard_map/while/body/eval_jaxpr/reduce_sum | solution.py:38
  143.8 1.0 constant_dynamic-slice_fusion.14
  144.8 3.7 fusion.45
  150.1 2.1 exponential_multiply_fusion.15
  152.3 10.2 %fusion.47 = (f32[3,32,128]{2,1,0:T(8,128)S(1)}, f32[32,128,128]{2,1,0:T(8,128)S(1)}, f32[32,128,128]{2,1,0:T(8,128)S(1)}, f32[32,128,128]{2,1,0:T(8,128)S(1)}, ...) fusion(f32[32,128,128]{2,1,0:T(8,128)S(1)} %get-tuple-element.2, ...), kind=kLoop, calls=%fused_computation.19.clone.1 | loop fusion | flops 34578432 | bytes 17317888 | tf_op jit(solution)/shard_map/while/body/eval_jaxpr/reduce_sum | solution.py:38
  164.2 14.1 %fusion.48 = (f32[3,32,128]{2,1,0:T(8,128)S(1)}, f32[3,32,128]{2,1,0:T(8,128)S(1)}, f32[3,32,128]{2,1,0:T(8,128)S(1)}, f32[3,32,128]{2,1,0:T(8,128)S(1)}, f32[3,...) fusion(f32[32,128,128]{2,1,0:T(8,128)S(1)} %exponential_multiply_fusion.16, ...), kind=kLoop, calls=%fused_computation.21.clone.1 | loop fusion | flops 28237824 | bytes 13221888 | tf_op jit(solution)/shard_map/while/body/eval_jaxpr/reduce_sum | solution.py:38
  188.7 3.7 fusion.45
  194.0 2.1 exponential_multiply_fusion.15
  196.2 10.2 %fusion.47 = (f32[3,32,128]{2,1,0:T(8,128)S(1)}, f32[32,128,128]{2,1,0:T(8,128)S(1)}, f32[32,128,128]{2,1,0:T(8,128)S(1)}, f32[32,128,128]{2,1,0:T(8,128)S(1)}, ...) fusion(f32[32,128,128]{2,1,0:T(8,128)S(1)} %get-tuple-element.2, ...), kind=kLoop, calls=%fused_computation.19.clone.1 | loop fusion | flops 34578432 | bytes 17317888 | tf_op jit(solution)/shard_map/while/body/eval_jaxpr/reduce_sum | solution.py:38
  208.1 14.1 %fusion.48 = (f32[3,32,128]{2,1,0:T(8,128)S(1)}, f32[3,32,128]{2,1,0:T(8,128)S(1)}, f32[3,32,128]{2,1,0:T(8,128)S(1)}, f32[3,32,128]{2,1,0:T(8,128)S(1)}, f32[3,...) fusion(f32[32,128,128]{2,1,0:T(8,128)S(1)} %exponential_multiply_fusion.16, ...), kind=kLoop, calls=%fused_computation.21.clone.1 | loop fusion | flops 28237824 | bytes 13221888 | tf_op jit(solution)/shard_map/while/body/eval_jaxpr/reduce_sum | solution.py:38
  231.6 1.0 constant_dynamic-slice_fusion.14
  232.6 3.7 fusion.45
  237.9 2.1 exponential_multiply_fusion.15
  240.1 10.2 %fusion.47 = (f32[3,32,128]{2,1,0:T(8,128)S(1)}, f32[32,128,128]{2,1,0:T(8,128)S(1)}, f32[32,128,128]{2,1,0:T(8,128)S(1)}, f32[32,128,128]{2,1,0:T(8,128)S(1)}, ...) fusion(f32[32,128,128]{2,1,0:T(8,128)S(1)} %get-tuple-element.2, ...), kind=kLoop, calls=%fused_computation.19.clone.1 | loop fusion | flops 34578432 | bytes 17317888 | tf_op jit(solution)/shard_map/while/body/eval_jaxpr/reduce_sum | solution.py:38
  252.0 14.1 %fusion.48 = (f32[3,32,128]{2,1,0:T(8,128)S(1)}, f32[3,32,128]{2,1,0:T(8,128)S(1)}, f32[3,32,128]{2,1,0:T(8,128)S(1)}, f32[3,32,128]{2,1,0:T(8,128)S(1)}, f32[3,...) fusion(f32[32,128,128]{2,1,0:T(8,128)S(1)} %exponential_multiply_fusion.16, ...), kind=kLoop, calls=%fused_computation.21.clone.1 | loop fusion | flops 28237824 | bytes 13221888 | tf_op jit(solution)/shard_map/while/body/eval_jaxpr/reduce_sum | solution.py:38
  275.5 1.0 constant_dynamic-slice_fusion.14
  276.6 3.7 fusion.45
  281.9 2.1 exponential_multiply_fusion.15
  284.0 10.2 %fusion.47 = (f32[3,32,128]{2,1,0:T(8,128)S(1)}, f32[32,128,128]{2,1,0:T(8,128)S(1)}, f32[32,128,128]{2,1,0:T(8,128)S(1)}, f32[32,128,128]{2,1,0:T(8,128)S(1)}, ...) fusion(f32[32,128,128]{2,1,0:T(8,128)S(1)} %get-tuple-element.2, ...), kind=kLoop, calls=%fused_computation.19.clone.1 | loop fusion | flops 34578432 | bytes 17317888 | tf_op jit(solution)/shard_map/while/body/eval_jaxpr/reduce_sum | solution.py:38
  296.0 14.1 %fusion.48 = (f32[3,32,128]{2,1,0:T(8,128)S(1)}, f32[3,32,128]{2,1,0:T(8,128)S(1)}, f32[3,32,128]{2,1,0:T(8,128)S(1)}, f32[3,32,128]{2,1,0:T(8,128)S(1)}, f32[3,...) fusion(f32[32,128,128]{2,1,0:T(8,128)S(1)} %exponential_multiply_fusion.16, ...), kind=kLoop, calls=%fused_computation.21.clone.1 | loop fusion | flops 28237824 | bytes 13221888 | tf_op jit(solution)/shard_map/while/body/eval_jaxpr/reduce_sum | solution.py:38
  319.4 1.0 constant_dynamic-slice_fusion.14
  320.5 3.7 fusion.45
  325.9 2.1 exponential_multiply_fusion.15
  328.0 10.2 %fusion.47 = (f32[3,32,128]{2,1,0:T(8,128)S(1)}, f32[32,128,128]{2,1,0:T(8,128)S(1)}, f32[32,128,128]{2,1,0:T(8,128)S(1)}, f32[32,128,128]{2,1,0:T(8,128)S(1)}, ...) fusion(f32[32,128,128]{2,1,0:T(8,128)S(1)} %get-tuple-element.2, ...), kind=kLoop, calls=%fused_computation.19.clone.1 | loop fusion | flops 34578432 | bytes 17317888 | tf_op jit(solution)/shard_map/while/body/eval_jaxpr/reduce_sum | solution.py:38
  339.9 14.1 %fusion.48 = (f32[3,32,128]{2,1,0:T(8,128)S(1)}, f32[3,32,128]{2,1,0:T(8,128)S(1)}, f32[3,32,128]{2,1,0:T(8,128)S(1)}, f32[3,32,128]{2,1,0:T(8,128)S(1)}, f32[3,...) fusion(f32[32,128,128]{2,1,0:T(8,128)S(1)} %exponential_multiply_fusion.16, ...), kind=kLoop, calls=%fused_computation.21.clone.1 | loop fusion | flops 28237824 | bytes 13221888 | tf_op jit(solution)/shard_map/while/body/eval_jaxpr/reduce_sum | solution.py:38
  363.4 1.1 constant_dynamic-slice_fusion.14
  364.5 3.7 fusion.45
  369.8 2.1 exponential_multiply_fusion.15
  372.0 10.2 %fusion.47 = (f32[3,32,128]{2,1,0:T(8,128)S(1)}, f32[32,128,128]{2,1,0:T(8,128)S(1)}, f32[32,128,128]{2,1,0:T(8,128)S(1)}, f32[32,128,128]{2,1,0:T(8,128)S(1)}, ...) fusion(f32[32,128,128]{2,1,0:T(8,128)S(1)} %get-tuple-element.2, ...), kind=kLoop, calls=%fused_computation.19.clone.1 | loop fusion | flops 34578432 | bytes 17317888 | tf_op jit(solution)/shard_map/while/body/eval_jaxpr/reduce_sum | solution.py:38
  383.9 14.1 %fusion.48 = (f32[3,32,128]{2,1,0:T(8,128)S(1)}, f32[3,32,128]{2,1,0:T(8,128)S(1)}, f32[3,32,128]{2,1,0:T(8,128)S(1)}, f32[3,32,128]{2,1,0:T(8,128)S(1)}, f32[3,...) fusion(f32[32,128,128]{2,1,0:T(8,128)S(1)} %exponential_multiply_fusion.16, ...), kind=kLoop, calls=%fused_computation.21.clone.1 | loop fusion | flops 28237824 | bytes 13221888 | tf_op jit(solution)/shard_map/while/body/eval_jaxpr/reduce_sum | solution.py:38
  398.7 1.0 bitcast_add_fusion
  399.8 1.9 collective-permute-start
  401.7 4.5 %collective-permute-start.1 = (f32[3,1,1024]{2,1,0:T(1,128)S(1)}, f32[3,1,1024]{2,1,0:T(1,128)S(1)}, u32[]{:S(2)}, u32[]{:S(2)}) collective-permute-start(f32[3,1,1024]{2,1,0:T(1,128)S(1)} %get-tuple-element.129), channel_id=1, source_target_pairs={{4,0},{8,4},{12,8},{16,12},{20,16},{24,20},{28,24},{5,1},{9,5},{13... | collective-permute-start | bytes 36872 | tf_op jit(solution)/shard_map/ppermute | solution.py:20
  407.9 9.6 %psum.7 = f32[33]{0:T(128)S(1)} all-reduce(f32[33]{0:T(128)S(1)} %fusion.22), channel_id=1, replica_groups=mesh['img'=8,'atom'=4] {'atom'}, use_global_device_ids=true, to_apply=%region_19.20 | all-reduce | flops 33 | bytes 264 | tf_op jit(solution)/shard_map/psum | solution.py:69
  418.2 1.3 bitcast_dynamic-update-slice_fusion.1
  420.1 12.4 %all-reduce = f32[8]{0:T(128)S(1)} all-reduce(f32[8]{0:T(128)S(1)} %bitcast_dynamic-update-slice_fusion.1), channel_id=2, replica_groups=mesh['img'=8,'atom'=4] {'img'}, use_global_device_ids=true, to_apply=%add | all-reduce | flops 8 | bytes 64 | tf_op jit(solution)/shard_map/all_gather | solution.py:75
  437.5 1.3 convolution_bitcast_fusion
  (136 shorter events, 51.6 us)
Async XLA Ops:
  6.5 40.6 %all-gather.3.cloned.1.call-start = ((), (), s32[]{:S(2)}) async-start(), calls=%async_computation | async-start | bytes 1966080 | tf_op jit(solution)/shard_map/all_gather | solution.py:58
  47.2 351.6 %copy-start = (f32[3,32,1024]{2,1,0:T(8,128)S(1)}, f32[3,32,1024]{2,1,0:T(8,128)}, u32[]{:S(2)}) copy-start(f32[3,32,1024]{2,1,0:T(8,128)} %param.6) | copy-start | bytes 1179652
  47.2 359.1 %copy-start.1 = (s32[32]{0:T(128)S(1)}, s32[32]{0:T(128)}, u32[]{:S(2)}) copy-start(s32[32]{0:T(128)} %param.9) | copy-start | bytes 388
  47.2 359.1 %copy-start.2 = (u32[32]{0:T(128)S(1)}, u32[32]{0:T(128)}, u32[]{:S(2)}) copy-start(u32[32]{0:T(128)} %constant.75) | copy-start | bytes 388
  399.8 7.1 %collective-permute-start = (f32[3,1,1024]{2,1,0:T(1,128)S(1)}, f32[3,1,1024]{2,1,0:T(1,128)S(1)}, u32[]{:S(2)}, u32[]{:S(2)}) collective-permute-start(f32[3,1,1024]{2,1,0:T(1,128)S(1)} %get-tuple-element.128), channel_id=1, source_target_pairs={{0,4},{4,8},{8,12},{12,16},{16,20},{20,24},{24,28},{1,5},{5,9},{9,... | collective-permute-start | bytes 36872 | tf_op jit(solution)/shard_map/ppermute | solution.py:18
  401.7 5.9 %collective-permute-start.1 = (f32[3,1,1024]{2,1,0:T(1,128)S(1)}, f32[3,1,1024]{2,1,0:T(1,128)S(1)}, u32[]{:S(2)}, u32[]{:S(2)}) collective-permute-start(f32[3,1,1024]{2,1,0:T(1,128)S(1)} %get-tuple-element.129), channel_id=1, source_target_pairs={{4,0},{8,4},{12,8},{16,12},{20,16},{24,20},{28,24},{5,1},{9,5},{13... | collective-permute-start | bytes 36872 | tf_op jit(solution)/shard_map/ppermute | solution.py:20
Sparse Core Ops, SparseCore 0:
  8.9 38.2 all-gather.2
where the time goes:
time: 448 us; the launch traced here: 446 us
  other arithmetic  264 us (59%)
  loops' own time  58.9 us (13%)
  waiting for transfers between devices  40.2 us (9%)
  local copies, waits for them, and re-layouts  36.3 us (8%)
  blocking collectives  22 us (5%)
  between operations  16.1 us (4%)
  starting transfers between devices  6.46 us (1%)
    reduce_sum x16, other arithmetic, pair_force(): force_sum = force_sum + jnp.sum(differ * coupling[None], axis=3)  194 us
    another operation x1, loops' own time, block_forces(): result = lax.map(one_block, (blocks, indices))  58.9 us
    all_gather x1, waiting for transfers between devices, shards(): whole_pos = lax.all_gather(positions, 'atom', axis=2, tiled=True)  38.8 us
    mul x64, other arithmetic, pair_force(): block_strength[None, :, None] * partner_strength[None, None, :]  31.5 us
    reduce_sum x8, other arithmetic, pair_force(): radius = jnp.sum(differ * differ, axis=0)  29.4 us
    all_gather x1, blocking collectives, shards(): totals = lax.all_gather(device_total[None], 'img', axis=0, tiled=True)  12.4 us
    psum x1, blocking collectives, shards(): squares = lax.psum(partial_value, 'atom')  9.62 us
  transfers between devices with their start and end apart: 3, of which 2 were waited for; matrix products, arithmetic and copies ran while one was open for 0% of the time, Pallas kernels for 0%

commit v1 on v0

--- a/solution.py
+++ b/solution.py
@@ -55,7 +55,12 @@
 def shards(positions, strength, tile_pairs, source_segment):
     count = positions.shape[1]
     local_atoms = positions.shape[2]
-    whole_pos = lax.all_gather(positions, "atom", axis=2, tiled=True)
+    ring = [positions]
+    for hop in range(3):
+        ring.append(lax.ppermute(ring[-1], "atom", [(dev, (dev + 1) % 4) for dev in range(4)]))
+    whole_pos = jnp.roll(
+        jnp.concatenate(ring[::-1], axis=2), (lax.axis_index("atom") + 1) * ring[0].shape[2], axis=2
+    )
     per_device = local_atoms // TB
     blocks = positions.reshape(3, count, per_device, TB).transpose(2, 0, 1, 3)
     indices = lax.axis_index("atom") * per_device + jnp.arange(per_device, dtype=jnp.int32)

time: 448 us -> 417 us (0.931)
  between operations: 16.1 us -> 2.75 us
  local copies, waits for them, and re-layouts: 36.3 us -> 24.4 us
  waiting for transfers between devices: 40.2 us -> 34 us
    all_gather x1 -> x0, waiting for transfers between devices: 38.8 us -> none  [shards(): whole_pos = lax.all_gather(positions, 'atom', axis=2, tiled=True)]
    ppermute x0 -> x3, waiting for transfers between devices: none -> 33.3 us  [shards(): lax.ppermute(ring[-1], 'atom', [(dev, (dev + 1) % 4) for dev in range(4)])]
    dynamic_slice x8, local copies, waits for them, and re-layouts: 8.23 us -> 0.58 us  [pair_force(): partner_pos = lax.dynamic_slice_in_dim(whole_pos, first_atom, TB, 2)]
    dynamic_slice x8, local copies, waits for them, and re-layouts: 6.1 us -> 0.59 us  [one_block(): partners = tile_pairs[index]]
  transfers between devices with their start and end apart: 3 -> 5, of which waited for: 2 -> 4; matrix products, arithmetic and copies ran while one was open for 0% -> 0% of each run, Pallas kernels for 0% -> 0%
where the time goes in v1:
time: 417 us; the launch traced here: 415 us
  other arithmetic  264 us (63%)
  loops' own time  59.1 us (14%)
  waiting for transfers between devices  34 us (8%)
  local copies, waits for them, and re-layouts  24.4 us (6%)
  blocking collectives  21 us (5%)
  starting transfers between devices  8.04 us (2%)
    reduce_sum x16, other arithmetic, pair_force(): force_sum = force_sum + jnp.sum(differ * coupling[None], axis=3)  194 us
    another operation x1, loops' own time, block_forces(): result = lax.map(one_block, (blocks, indices))  59.1 us
    ppermute x3, waiting for transfers between devices, shards(): lax.ppermute(ring[-1], 'atom', [(dev, (dev + 1) % 4) for dev in range(4)])  33.3 us
    mul x64, other arithmetic, pair_force(): block_strength[None, :, None] * partner_strength[None, None, :]  31.5 us
    reduce_sum x8, other arithmetic, pair_force(): radius = jnp.sum(differ * differ, axis=0)  29.4 us
    all_gather x1, blocking collectives, shards(): totals = lax.all_gather(device_total[None], 'img', axis=0, tiled=True)  12.6 us
    psum x1, blocking collectives, shards(): squares = lax.psum(partial_value, 'atom')  8.44 us
  transfers between devices with their start and end apart: 5, of which 4 were waited for; matrix products, arithmetic and copies ran while one was open for 0% of the time, Pallas kernels for 0%

profile of v1, /device:TPU:4, one launch (start us, length us, event | category | flops | bytes accessed | tf_op | source)
XLA Modules:
  0.0 415.1 jit_solution(17208141507518555670)
XLA Ops:
  0.0 1.6 collective-permute-start
  1.6 11.4 %collective-permute-done = f32[3,32,1024]{2,1,0:T(8,128)S(1)} collective-permute-done((f32[3,32,1024]{2,1,0:T(8,128)}, f32[3,32,1024]{2,1,0:T(8,128)S(1)}, u32[]{:S(2)}, u32[]{:S(2)}) %collective-permute-start) | collective-permute-done | bytes 393248 | tf_op jit(solution)/shard_map/ppermute | solution.py:60
  13.0 11.9 %collective-permute-done.1 = f32[3,32,1024]{2,1,0:T(8,128)S(1)} collective-permute-done((f32[3,32,1024]{2,1,0:T(8,128)S(1)}, f32[3,32,1024]{2,1,0:T(8,128)S(1)}, u32[]{:S(2)}, u32[]{:S(2)}) %collective-permute-start.1) | collective-permute-done | bytes 393248 | tf_op jit(solution)/shard_map/ppermute | solution.py:60
  24.9 1.1 copy.15
  26.1 9.9 %collective-permute-done.2 = f32[3,32,1024]{2,1,0:T(8,128)S(1)} collective-permute-done((f32[3,32,1024]{2,1,0:T(8,128)S(1)}, f32[3,32,1024]{2,1,0:T(8,128)S(1)}, u32[]{:S(2)}, u32[]{:S(2)}) %collective-permute-start.2) | collective-permute-done | bytes 393248 | tf_op jit(solution)/shard_map/ppermute | solution.py:60
  36.8 339.1 %while.10 = (s32[]{:T(128)}, f32[8,3,32,128]{3,2,1,0:T(8,128)}, f32[8,3,32,128]{3,0,2,1:T(8,128)S(1)}, s32[8]{0:T(128)S(1)}, s32[32,8]{0,1:T(8,128)S(1)}, /*inde...) while((s32[]{:T(128)}, f32[8,3,32,128]{3,2,1,0:T(8,128)}, ...), condition=%wide.region_17.18_spmd, body=%wide.region_0.17_spmd.sunk | while | flops 79810600 | bytes 83409736 | solution.py:50
  45.0 3.7 fusion.45
  49.2 1.0 fusion.46
  50.4 2.1 exponential_multiply_fusion.15
  52.5 10.2 %fusion.47 = (f32[3,32,128]{2,1,0:T(8,128)S(1)}, f32[32,128,128]{2,1,0:T(8,128)S(1)}, f32[32,128,128]{2,1,0:T(8,128)S(1)}, f32[32,128,128]{2,1,0:T(8,128)S(1)}, ...) fusion(f32[32,128,128]{2,1,0:T(8,128)S(1)} %get-tuple-element.2, ...), kind=kLoop, calls=%fused_computation.19.clone.1 | loop fusion | flops 34578432 | bytes 17317888 | tf_op jit(solution)/shard_map/while/body/eval_jaxpr/reduce_sum | solution.py:38
  64.4 14.1 %fusion.48 = (f32[3,32,128]{2,1,0:T(8,128)S(1)}, f32[3,32,128]{2,1,0:T(8,128)S(1)}, f32[3,32,128]{2,1,0:T(8,128)S(1)}, f32[3,32,128]{2,1,0:T(8,128)S(1)}, f32[3,...) fusion(f32[32,128,128]{2,1,0:T(8,128)S(1)} %exponential_multiply_fusion.16, ...), kind=kLoop, calls=%fused_computation.21.clone.1 | loop fusion | flops 28237824 | bytes 13221888 | tf_op jit(solution)/shard_map/while/body/eval_jaxpr/reduce_sum | solution.py:38
  87.4 3.7 fusion.45
  92.7 2.1 exponential_multiply_fusion.15
  94.9 10.2 %fusion.47 = (f32[3,32,128]{2,1,0:T(8,128)S(1)}, f32[32,128,128]{2,1,0:T(8,128)S(1)}, f32[32,128,128]{2,1,0:T(8,128)S(1)}, f32[32,128,128]{2,1,0:T(8,128)S(1)}, ...) fusion(f32[32,128,128]{2,1,0:T(8,128)S(1)} %get-tuple-element.2, ...), kind=kLoop, calls=%fused_computation.19.clone.1 | loop fusion | flops 34578432 | bytes 17317888 | tf_op jit(solution)/shard_map/while/body/eval_jaxpr/reduce_sum | solution.py:38
  106.8 14.1 %fusion.48 = (f32[3,32,128]{2,1,0:T(8,128)S(1)}, f32[3,32,128]{2,1,0:T(8,128)S(1)}, f32[3,32,128]{2,1,0:T(8,128)S(1)}, f32[3,32,128]{2,1,0:T(8,128)S(1)}, f32[3,...) fusion(f32[32,128,128]{2,1,0:T(8,128)S(1)} %exponential_multiply_fusion.16, ...), kind=kLoop, calls=%fused_computation.21.clone.1 | loop fusion | flops 28237824 | bytes 13221888 | tf_op jit(solution)/shard_map/while/body/eval_jaxpr/reduce_sum | solution.py:38
  129.8 3.7 fusion.45
  135.1 2.1 exponential_multiply_fusion.15
  137.3 10.2 %fusion.47 = (f32[3,32,128]{2,1,0:T(8,128)S(1)}, f32[32,128,128]{2,1,0:T(8,128)S(1)}, f32[32,128,128]{2,1,0:T(8,128)S(1)}, f32[32,128,128]{2,1,0:T(8,128)S(1)}, ...) fusion(f32[32,128,128]{2,1,0:T(8,128)S(1)} %get-tuple-element.2, ...), kind=kLoop, calls=%fused_computation.19.clone.1 | loop fusion | flops 34578432 | bytes 17317888 | tf_op jit(solution)/shard_map/while/body/eval_jaxpr/reduce_sum | solution.py:38
  149.2 14.1 %fusion.48 = (f32[3,32,128]{2,1,0:T(8,128)S(1)}, f32[3,32,128]{2,1,0:T(8,128)S(1)}, f32[3,32,128]{2,1,0:T(8,128)S(1)}, f32[3,32,128]{2,1,0:T(8,128)S(1)}, f32[3,...) fusion(f32[32,128,128]{2,1,0:T(8,128)S(1)} %exponential_multiply_fusion.16, ...), kind=kLoop, calls=%fused_computation.21.clone.1 | loop fusion | flops 28237824 | bytes 13221888 | tf_op jit(solution)/shard_map/while/body/eval_jaxpr/reduce_sum | solution.py:38
  172.2 3.7 fusion.45
  177.5 2.1 exponential_multiply_fusion.15
  179.6 10.2 %fusion.47 = (f32[3,32,128]{2,1,0:T(8,128)S(1)}, f32[32,128,128]{2,1,0:T(8,128)S(1)}, f32[32,128,128]{2,1,0:T(8,128)S(1)}, f32[32,128,128]{2,1,0:T(8,128)S(1)}, ...) fusion(f32[32,128,128]{2,1,0:T(8,128)S(1)} %get-tuple-element.2, ...), kind=kLoop, calls=%fused_computation.19.clone.1 | loop fusion | flops 34578432 | bytes 17317888 | tf_op jit(solution)/shard_map/while/body/eval_jaxpr/reduce_sum | solution.py:38
  191.6 14.1 %fusion.48 = (f32[3,32,128]{2,1,0:T(8,128)S(1)}, f32[3,32,128]{2,1,0:T(8,128)S(1)}, f32[3,32,128]{2,1,0:T(8,128)S(1)}, f32[3,32,128]{2,1,0:T(8,128)S(1)}, f32[3,...) fusion(f32[32,128,128]{2,1,0:T(8,128)S(1)} %exponential_multiply_fusion.16, ...), kind=kLoop, calls=%fused_computation.21.clone.1 | loop fusion | flops 28237824 | bytes 13221888 | tf_op jit(solution)/shard_map/while/body/eval_jaxpr/reduce_sum | solution.py:38
  214.6 3.7 fusion.45
  219.9 2.1 exponential_multiply_fusion.15
  222.0 10.2 %fusion.47 = (f32[3,32,128]{2,1,0:T(8,128)S(1)}, f32[32,128,128]{2,1,0:T(8,128)S(1)}, f32[32,128,128]{2,1,0:T(8,128)S(1)}, f32[32,128,128]{2,1,0:T(8,128)S(1)}, ...) fusion(f32[32,128,128]{2,1,0:T(8,128)S(1)} %get-tuple-element.2, ...), kind=kLoop, calls=%fused_computation.19.clone.1 | loop fusion | flops 34578432 | bytes 17317888 | tf_op jit(solution)/shard_map/while/body/eval_jaxpr/reduce_sum | solution.py:38
  233.9 14.1 %fusion.48 = (f32[3,32,128]{2,1,0:T(8,128)S(1)}, f32[3,32,128]{2,1,0:T(8,128)S(1)}, f32[3,32,128]{2,1,0:T(8,128)S(1)}, f32[3,32,128]{2,1,0:T(8,128)S(1)}, f32[3,...) fusion(f32[32,128,128]{2,1,0:T(8,128)S(1)} %exponential_multiply_fusion.16, ...), kind=kLoop, calls=%fused_computation.21.clone.1 | loop fusion | flops 28237824 | bytes 13221888 | tf_op jit(solution)/shard_map/while/body/eval_jaxpr/reduce_sum | solution.py:38
  257.0 3.7 fusion.45
  261.2 1.0 fusion.46
  262.3 2.1 exponential_multiply_fusion.15
  264.4 10.2 %fusion.47 = (f32[3,32,128]{2,1,0:T(8,128)S(1)}, f32[32,128,128]{2,1,0:T(8,128)S(1)}, f32[32,128,128]{2,1,0:T(8,128)S(1)}, f32[32,128,128]{2,1,0:T(8,128)S(1)}, ...) fusion(f32[32,128,128]{2,1,0:T(8,128)S(1)} %get-tuple-element.2, ...), kind=kLoop, calls=%fused_computation.19.clone.1 | loop fusion | flops 34578432 | bytes 17317888 | tf_op jit(solution)/shard_map/while/body/eval_jaxpr/reduce_sum | solution.py:38
  276.4 14.1 %fusion.48 = (f32[3,32,128]{2,1,0:T(8,128)S(1)}, f32[3,32,128]{2,1,0:T(8,128)S(1)}, f32[3,32,128]{2,1,0:T(8,128)S(1)}, f32[3,32,128]{2,1,0:T(8,128)S(1)}, f32[3,...) fusion(f32[32,128,128]{2,1,0:T(8,128)S(1)} %exponential_multiply_fusion.16, ...), kind=kLoop, calls=%fused_computation.21.clone.1 | loop fusion | flops 28237824 | bytes 13221888 | tf_op jit(solution)/shard_map/while/body/eval_jaxpr/reduce_sum | solution.py:38
  299.4 3.7 fusion.45
  303.6 1.0 fusion.46
  304.7 2.1 exponential_multiply_fusion.15
  306.9 10.2 %fusion.47 = (f32[3,32,128]{2,1,0:T(8,128)S(1)}, f32[32,128,128]{2,1,0:T(8,128)S(1)}, f32[32,128,128]{2,1,0:T(8,128)S(1)}, f32[32,128,128]{2,1,0:T(8,128)S(1)}, ...) fusion(f32[32,128,128]{2,1,0:T(8,128)S(1)} %get-tuple-element.2, ...), kind=kLoop, calls=%fused_computation.19.clone.1 | loop fusion | flops 34578432 | bytes 17317888 | tf_op jit(solution)/shard_map/while/body/eval_jaxpr/reduce_sum | solution.py:38
  318.8 14.1 %fusion.48 = (f32[3,32,128]{2,1,0:T(8,128)S(1)}, f32[3,32,128]{2,1,0:T(8,128)S(1)}, f32[3,32,128]{2,1,0:T(8,128)S(1)}, f32[3,32,128]{2,1,0:T(8,128)S(1)}, f32[3,...) fusion(f32[32,128,128]{2,1,0:T(8,128)S(1)} %exponential_multiply_fusion.16, ...), kind=kLoop, calls=%fused_computation.21.clone.1 | loop fusion | flops 28237824 | bytes 13221888 | tf_op jit(solution)/shard_map/while/body/eval_jaxpr/reduce_sum | solution.py:38
  341.8 3.7 fusion.45
  347.1 2.1 exponential_multiply_fusion.15
  349.2 10.2 %fusion.47 = (f32[3,32,128]{2,1,0:T(8,128)S(1)}, f32[32,128,128]{2,1,0:T(8,128)S(1)}, f32[32,128,128]{2,1,0:T(8,128)S(1)}, f32[32,128,128]{2,1,0:T(8,128)S(1)}, ...) fusion(f32[32,128,128]{2,1,0:T(8,128)S(1)} %get-tuple-element.2, ...), kind=kLoop, calls=%fused_computation.19.clone.1 | loop fusion | flops 34578432 | bytes 17317888 | tf_op jit(solution)/shard_map/while/body/eval_jaxpr/reduce_sum | solution.py:38
  361.2 14.1 %fusion.48 = (f32[3,32,128]{2,1,0:T(8,128)S(1)}, f32[3,32,128]{2,1,0:T(8,128)S(1)}, f32[3,32,128]{2,1,0:T(8,128)S(1)}, f32[3,32,128]{2,1,0:T(8,128)S(1)}, f32[3,...) fusion(f32[32,128,128]{2,1,0:T(8,128)S(1)} %exponential_multiply_fusion.16, ...), kind=kLoop, calls=%fused_computation.21.clone.1 | loop fusion | flops 28237824 | bytes 13221888 | tf_op jit(solution)/shard_map/while/body/eval_jaxpr/reduce_sum | solution.py:38
  376.0 1.0 bitcast_add_fusion
  377.1 1.9 collective-permute-start.3
  379.0 4.5 %collective-permute-start.4 = (f32[3,1,1024]{2,1,0:T(1,128)S(1)}, f32[3,1,1024]{2,1,0:T(1,128)S(1)}, u32[]{:S(2)}, u32[]{:S(2)}) collective-permute-start(f32[3,1,1024]{2,1,0:T(1,128)S(1)} %get-tuple-element.129), channel_id=1, source_target_pairs={{4,0},{8,4},{12,8},{16,12},{20,16},{24,20},{28,24},{5,1},{9,5},{13... | collective-permute-start | bytes 36872 | tf_op jit(solution)/shard_map/ppermute | solution.py:20
  385.1 8.4 %psum.7 = f32[33]{0:T(128)S(1)} all-reduce(f32[33]{0:T(128)S(1)} %fusion.22), channel_id=1, replica_groups=mesh['img'=8,'atom'=4] {'atom'}, use_global_device_ids=true, to_apply=%region_19.20 | all-reduce | flops 33 | bytes 264 | tf_op jit(solution)/shard_map/psum | solution.py:74
  394.3 1.3 bitcast_dynamic-update-slice_fusion.1
  396.2 12.6 %all-reduce = f32[8]{0:T(128)S(1)} all-reduce(f32[8]{0:T(128)S(1)} %bitcast_dynamic-update-slice_fusion.1), channel_id=2, replica_groups=mesh['img'=8,'atom'=4] {'img'}, use_global_device_ids=true, to_apply=%add | all-reduce | flops 8 | bytes 64 | tf_op jit(solution)/shard_map/all_gather | solution.py:80
  413.8 1.3 convolution_bitcast_fusion
  (182 shorter events, 42.2 us)
Async XLA Ops:
  0.0 36.1 %copy-start.2 = (f32[3,32,1024]{2,1,0:T(8,128)S(1)}, f32[3,32,1024]{2,1,0:T(8,128)}, u32[]{:S(2)}) copy-start(f32[3,32,1024]{2,1,0:T(8,128)} %param.6) | copy-start | bytes 1179652
  0.0 13.0 %collective-permute-start = (f32[3,32,1024]{2,1,0:T(8,128)}, f32[3,32,1024]{2,1,0:T(8,128)S(1)}, u32[]{:S(2)}, u32[]{:S(2)}) collective-permute-start(f32[3,32,1024]{2,1,0:T(8,128)} %param.6), channel_id=1, source_target_pairs={{0,1},{1,2},{2,3},{3,0},{4,5},{5,6},{6,7},{7,4},{8,9},{9,10},{10,1... | collective-permute-start | bytes 1179656 | tf_op jit(solution)/shard_map/ppermute | solution.py:60
  13.0 11.9 %collective-permute-start.1 = (f32[3,32,1024]{2,1,0:T(8,128)S(1)}, f32[3,32,1024]{2,1,0:T(8,128)S(1)}, u32[]{:S(2)}, u32[]{:S(2)}) collective-permute-start(f32[3,32,1024]{2,1,0:T(8,128)S(1)} %collective-permute-done), channel_id=1, source_target_pairs={{0,1},{1,2},{2,3},{3,0},{4,5},{5,6},{6,7},{7,4},{8,9},{9,10},{10,1... | collective-permute-start | bytes 1179656 | tf_op jit(solution)/shard_map/ppermute | solution.py:60
  24.9 11.1 %collective-permute-start.2 = (f32[3,32,1024]{2,1,0:T(8,128)S(1)}, f32[3,32,1024]{2,1,0:T(8,128)S(1)}, u32[]{:S(2)}, u32[]{:S(2)}) collective-permute-start(f32[3,32,1024]{2,1,0:T(8,128)S(1)} %collective-permute-done.1), channel_id=1, source_target_pairs={{0,1},{1,2},{2,3},{3,0},{4,5},{5,6},{6,7},{7,4},{8,9},{9,10},{10,1... | collective-permute-start | bytes 1179656 | tf_op jit(solution)/shard_map/ppermute | solution.py:60
  36.2 0.7 copy-start.3
  36.8 346.7 %copy-start.4 = (s32[32]{0:T(128)S(1)}, s32[32]{0:T(128)}, u32[]{:S(2)}) copy-start(s32[32]{0:T(128)} %param.9) | copy-start | bytes 388
  36.8 346.7 %copy-start.5 = (u32[32]{0:T(128)S(1)}, u32[32]{0:T(128)}, u32[]{:S(2)}) copy-start(u32[32]{0:T(128)} %constant.99) | copy-start | bytes 388
  36.8 8.1 %copy-start = (f32[3,32,4096]{2,1,0:T(8,128)}, f32[3,32,4096]{2,1,0:T(8,128)S(1)}, u32[]{:S(2)}) copy-start(f32[3,32,4096]{2,1,0:T(8,128)S(1)} %get-tuple-element.308) | copy-start | bytes 4718596 | tf_op jit(solution)/shard_map/while
  64.4 14.8 %copy-start.1 = (f32[3,32,4096]{2,1,0:T(8,128)S(1)}, f32[3,32,4096]{2,1,0:T(8,128)}, u32[]{:S(2)}) copy-start(f32[3,32,4096]{2,1,0:T(8,128)} %copy-done) | copy-start | bytes 4718596 | tf_op jit(solution)/shard_map/while
  79.2 8.2 %copy-start = (f32[3,32,4096]{2,1,0:T(8,128)}, f32[3,32,4096]{2,1,0:T(8,128)S(1)}, u32[]{:S(2)}) copy-start(f32[3,32,4096]{2,1,0:T(8,128)S(1)} %get-tuple-element.308) | copy-start | bytes 4718596 | tf_op jit(solution)/shard_map/while
  106.8 14.8 %copy-start.1 = (f32[3,32,4096]{2,1,0:T(8,128)S(1)}, f32[3,32,4096]{2,1,0:T(8,128)}, u32[]{:S(2)}) copy-start(f32[3,32,4096]{2,1,0:T(8,128)} %copy-done) | copy-start | bytes 4718596 | tf_op jit(solution)/shard_map/while
  121.6 8.2 %copy-start = (f32[3,32,4096]{2,1,0:T(8,128)}, f32[3,32,4096]{2,1,0:T(8,128)S(1)}, u32[]{:S(2)}) copy-start(f32[3,32,4096]{2,1,0:T(8,128)S(1)} %get-tuple-element.308) | copy-start | bytes 4718596 | tf_op jit(solution)/shard_map/while
  149.2 14.8 %copy-start.1 = (f32[3,32,4096]{2,1,0:T(8,128)S(1)}, f32[3,32,4096]{2,1,0:T(8,128)}, u32[]{:S(2)}) copy-start(f32[3,32,4096]{2,1,0:T(8,128)} %copy-done) | copy-start | bytes 4718596 | tf_op jit(solution)/shard_map/while
  164.0 8.2 %copy-start = (f32[3,32,4096]{2,1,0:T(8,128)}, f32[3,32,4096]{2,1,0:T(8,128)S(1)}, u32[]{:S(2)}) copy-start(f32[3,32,4096]{2,1,0:T(8,128)S(1)} %get-tuple-element.308) | copy-start | bytes 4718596 | tf_op jit(solution)/shard_map/while
  191.5 14.8 %copy-start.1 = (f32[3,32,4096]{2,1,0:T(8,128)S(1)}, f32[3,32,4096]{2,1,0:T(8,128)}, u32[]{:S(2)}) copy-start(f32[3,32,4096]{2,1,0:T(8,128)} %copy-done) | copy-start | bytes 4718596 | tf_op jit(solution)/shard_map/while
  206.4 8.2 %copy-start = (f32[3,32,4096]{2,1,0:T(8,128)}, f32[3,32,4096]{2,1,0:T(8,128)S(1)}, u32[]{:S(2)}) copy-start(f32[3,32,4096]{2,1,0:T(8,128)S(1)} %get-tuple-element.308) | copy-start | bytes 4718596 | tf_op jit(solution)/shard_map/while
  233.9 14.8 %copy-start.1 = (f32[3,32,4096]{2,1,0:T(8,128)S(1)}, f32[3,32,4096]{2,1,0:T(8,128)}, u32[]{:S(2)}) copy-start(f32[3,32,4096]{2,1,0:T(8,128)} %copy-done) | copy-start | bytes 4718596 | tf_op jit(solution)/shard_map/while
  248.7 8.2 %copy-start = (f32[3,32,4096]{2,1,0:T(8,128)}, f32[3,32,4096]{2,1,0:T(8,128)S(1)}, u32[]{:S(2)}) copy-start(f32[3,32,4096]{2,1,0:T(8,128)S(1)} %get-tuple-element.308) | copy-start | bytes 4718596 | tf_op jit(solution)/shard_map/while
  276.3 14.8 %copy-start.1 = (f32[3,32,4096]{2,1,0:T(8,128)S(1)}, f32[3,32,4096]{2,1,0:T(8,128)}, u32[]{:S(2)}) copy-start(f32[3,32,4096]{2,1,0:T(8,128)} %copy-done) | copy-start | bytes 4718596 | tf_op jit(solution)/shard_map/while
  291.2 8.2 %copy-start = (f32[3,32,4096]{2,1,0:T(8,128)}, f32[3,32,4096]{2,1,0:T(8,128)S(1)}, u32[]{:S(2)}) copy-start(f32[3,32,4096]{2,1,0:T(8,128)S(1)} %get-tuple-element.308) | copy-start | bytes 4718596 | tf_op jit(solution)/shard_map/while
  318.8 14.8 %copy-start.1 = (f32[3,32,4096]{2,1,0:T(8,128)S(1)}, f32[3,32,4096]{2,1,0:T(8,128)}, u32[]{:S(2)}) copy-start(f32[3,32,4096]{2,1,0:T(8,128)} %copy-done) | copy-start | bytes 4718596 | tf_op jit(solution)/shard_map/while
  333.6 8.2 %copy-start = (f32[3,32,4096]{2,1,0:T(8,128)}, f32[3,32,4096]{2,1,0:T(8,128)S(1)}, u32[]{:S(2)}) copy-start(f32[3,32,4096]{2,1,0:T(8,128)S(1)} %get-tuple-element.308) | copy-start | bytes 4718596 | tf_op jit(solution)/shard_map/while
  361.2 14.8 %copy-start.1 = (f32[3,32,4096]{2,1,0:T(8,128)S(1)}, f32[3,32,4096]{2,1,0:T(8,128)}, u32[]{:S(2)}) copy-start(f32[3,32,4096]{2,1,0:T(8,128)} %copy-done) | copy-start | bytes 4718596 | tf_op jit(solution)/shard_map/while
  377.1 7.1 %collective-permute-start.3 = (f32[3,1,1024]{2,1,0:T(1,128)S(1)}, f32[3,1,1024]{2,1,0:T(1,128)S(1)}, u32[]{:S(2)}, u32[]{:S(2)}) collective-permute-start(f32[3,1,1024]{2,1,0:T(1,128)S(1)} %get-tuple-element.128), channel_id=1, source_target_pairs={{0,4},{4,8},{8,12},{12,16},{16,20},{20,24},{24,28},{1,5},{5,9},{9,... | collective-permute-start | bytes 36872 | tf_op jit(solution)/shard_map/ppermute | solution.py:18
  379.0 5.9 %collective-permute-start.4 = (f32[3,1,1024]{2,1,0:T(1,128)S(1)}, f32[3,1,1024]{2,1,0:T(1,128)S(1)}, u32[]{:S(2)}, u32[]{:S(2)}) collective-permute-start(f32[3,1,1024]{2,1,0:T(1,128)S(1)} %get-tuple-element.129), channel_id=1, source_target_pairs={{4,0},{8,4},{12,8},{16,12},{20,16},{24,20},{28,24},{5,1},{9,5},{13... | collective-permute-start | bytes 36872 | tf_op jit(solution)/shard_map/ppermute | solution.py:20
